TPU v7x, 32 devices: a whole 2x2x4 slice. The times are simulated.
32 devices in a mesh: grp: 2 (over y), gx: 4 (over z), gy: 2 (over x), gz: 2 (over core).
Axes of the slice: x: 2, y: 2, z: 4, core: 2. Of those that a mesh axis runs over, the one named last changes fastest.
Arguments:
- observed: float32 [2048, 4, 256], P(('grp', 'gx', 'gy', 'gz')), parts along dimension 0, may hold values from -12 to 12
- predicted: float32 [2048, 4, 256], P(('grp', 'gx', 'gy', 'gz')), parts along dimension 0, may hold values from -6 to 6
- coherence_mask: int32 [2048, 256], P(('grp', 'gx', 'gy', 'gz')), parts along dimension 0, may hold values 0 or 1
- block_count: int32 [2048], P(('grp', 'gx', 'gy', 'gz')), parts along dimension 0, may hold values from 64 to 256
- block_owner: int32 [2048, 1], P(('grp', 'gx', 'gy', 'gz')), parts along dimension 0, may hold values from 0 to 7; in each aligned block of 64 rows (0 to 63, 64 to 127, ...) at most 16 rows name the same one
- block_matrix_choice: int32 [2048], P(('grp', 'gx', 'gy', 'gz')), parts along dimension 0, may hold values from 0 to 31
- block_patch: int32 [2048], P(('grp', 'gx', 'gy', 'gz')), parts along dimension 0, may hold values from 0 to 31
- look_vector: float32 [4, 3], replicated, may hold values from -1 to 1
- interp_weights: bfloat16 [32, 256, 128], replicated, may hold values from -0.375 to 0.375
- depth_kernel: float32 [64], P(('grp', 'gz')), parts along dimension 0, may hold values from 0.2 to 1
- stiffness: float32 [64, 128, 256], P(('grp', 'gz'), 'gx', 'gy'), parts along dimension 0, may hold values from 0.25 to 4
Outputs:
- adjoint_field: float32 [3, 64, 128, 256], P(None, ('grp', 'gz'), 'gx', 'gy'), parts along dimension 1
- cg_residual: float32 [3, 64, 128, 256], P(None, ('grp', 'gz'), 'gx', 'gy'), parts along dimension 1
There are 2 independent parts, one for each index of `grp`. A program takes and returns all parts, laid end to end along the dimension named above; an argument that names none is the same for every part. Nothing has to cross between parts.
Inputs may be any that keep to these rules, and one draw needn't show every extreme that they name: `block_owner`: the blocks of one device name no column tile more than 16 times; in some devices one tile is named exactly 16 times.
All inputs are finite; a program needn't handle non-finite values. No bound on the sum of `coherence_mask` on one device may be relied on, other than what follows from the above.
Results may differ from a plain program's by a relative error of at most 0.0029.
Values sent between devices are 32-bit elements; how exact they have to be, the bound alone decides.
A program may use at most 64 MiB of HBM per device.

v0:
```python
import math
import jax
import jax.numpy as jnp
from jax import lax
from jax.sharding import PartitionSpec as P

EPOCHS = 4
PATCH_X = 8
PATCH_Y = 16
ITERS = 3
KAPPA = 0.5
EPS = 1e-06
SPATIAL = (1, 2, 0)


def extended(cells, sides, width):
    for axis, dim in sides:
        count = lax.axis_size(axis)
        ends = count - 1
        head = lax.slice_in_dim(cells, 0, width, axis=dim)
        tail = lax.slice_in_dim(cells, cells.shape[dim] - width, cells.shape[dim], axis=dim)
        cells = jnp.concatenate(
            [
                lax.ppermute(tail, axis, [(i, (i + 1) % count) for i in range(ends)]),
                cells,
                lax.ppermute(head, axis, [((i + 1) % count, i) for i in range(ends)]),
            ],
            axis=dim,
        )
    return cells


def beside_all(padded):
    total = padded[2:, 1:-1, 1:-1] + padded[:-2, 1:-1, 1:-1]
    total = total + padded[1:-1, 2:, 1:-1] + padded[1:-1, :-2, 1:-1]
    return total + padded[1:-1, 1:-1, 2:] + padded[1:-1, 1:-1, :-2]


def central(padded, axis):
    if axis == 0:
        return 0.5 * (padded[2:, 1:-1, 1:-1] - padded[:-2, 1:-1, 1:-1])
    if axis == 1:
        return 0.5 * (padded[1:-1, 2:, 1:-1] - padded[1:-1, :-2, 1:-1])
    return 0.5 * (padded[1:-1, 1:-1, 2:] - padded[1:-1, 1:-1, :-2])


def operate(field, stiffness):
    padded = extended(field, (("gx", 2), ("gy", 3), ("gz", 1)), 1)
    spread = (
        central(padded[0], SPATIAL[0])
        + central(padded[1], SPATIAL[1])
        + central(padded[2], SPATIAL[2])
    )
    spread_pad = extended(spread, (("gx", 1), ("gy", 2), ("gz", 0)), 1)
    parts = [
        (6.0 + stiffness) * field[member]
        - beside_all(padded[member])
        - KAPPA * central(spread_pad, SPATIAL[member])
        for member in range(3)
    ]
    return jnp.stack(parts)


def project(resid, look_vector):
    return jnp.einsum("ec,nep->ncp", look_vector, resid, precision=lax.Precision.HIGHEST).astype(
        jnp.bfloat16
    )


def contribute(coeffs, tables, weights):
    total = coeffs.shape[0]
    group = math.gcd(total, 32)
    coefficient_sets = coeffs.reshape(total // group, group, 3, coeffs.shape[2])
    table_groups = tables.reshape(total // group, group)

    def per_group(both_parts):
        block_coefficient_values, block_tables = both_parts
        selected_entries = jnp.take(weights, block_tables, axis=0)
        return jnp.einsum(
            "aow,awv->aov",
            block_coefficient_values,
            selected_entries,
            preferred_element_type=jnp.float32,
        )

    result = lax.map(per_group, (coefficient_sets, table_groups))
    return result.reshape(total, 3, weights.shape[2])


def two_products(residual, image):
    return lax.psum((jnp.sum(residual * residual), jnp.sum(residual * image)), ("gx", "gy", "gz"))


def per_device(
    observed,
    predicted,
    coherence_mask,
    block_count,
    block_owner,
    block_matrix_choice,
    block_patch,
    look_vector,
    interp_weights,
    depth_kernel,
    stiffness,
):
    blocks = observed.shape[0]
    pixels = observed.shape[2]
    cells = PATCH_X * PATCH_Y
    owners = lax.axis_size("gx") * lax.axis_size("gy")
    capacity = max(4, 2 * blocks // owners)
    slots = owners * capacity
    local_x = stiffness.shape[1]
    local_y = stiffness.shape[2]
    places_x = local_x // PATCH_X
    northing_places = local_y // PATCH_Y
    places = places_x * northing_places
    column = lax.broadcasted_iota(jnp.int32, (blocks, pixels), 1)
    valid = coherence_mask.astype(jnp.float32) * (column < block_count[:, None]).astype(jnp.float32)
    resid = (predicted - observed) * valid[:, None, :]
    misfit, weight = lax.psum((jnp.sum(resid * resid), jnp.sum(valid)), ("gx", "gy", "gz"))
    scale = lax.rsqrt(misfit / (EPOCHS * weight) + EPS)
    owner = block_owner[:, 0]
    order = lax.broadcasted_iota(jnp.int32, (blocks, blocks), 0)
    other = lax.broadcasted_iota(jnp.int32, (blocks, blocks), 1)
    earlier = (owner[:, None] == owner[None, :]) & (other < order)
    rank = jnp.sum(earlier.astype(jnp.int32), axis=1)
    slot = owner * capacity + rank
    slot_ids = lax.broadcasted_iota(jnp.int32, (blocks, slots), 1)
    chosen = slot_ids == slot[:, None]
    select = chosen.astype(jnp.float32)
    patch_slot = jnp.sum(jnp.where(chosen, block_patch[:, None], 0), axis=0).reshape(
        owners, capacity
    )
    table_slot = jnp.sum(jnp.where(chosen, block_matrix_choice[:, None], 0), axis=0).reshape(
        owners, capacity
    )
    resid_slot = jnp.einsum("bs,bep->sep", select, resid, precision=lax.Precision.HIGHEST).reshape(
        owners, capacity, EPOCHS, pixels
    )
    arrived = lax.all_to_all(resid_slot, ("gx", "gy"), split_axis=0, concat_axis=0, tiled=True)
    tables = lax.all_to_all(table_slot, ("gx", "gy"), split_axis=0, concat_axis=0, tiled=True)
    patches = lax.all_to_all(patch_slot, ("gx", "gy"), split_axis=0, concat_axis=0, tiled=True)
    sources = tables.shape[0]
    width = tables.shape[1]
    coeffs = project(arrived.reshape(sources * width, EPOCHS, pixels), look_vector)
    sums = contribute(coeffs, tables.reshape(sources * width), interp_weights)
    patch_total_sums = sums.reshape(sources, width, 3, cells)
    flat_sums = patch_total_sums.reshape(slots, 3, cells)
    flat_ids = patches.reshape(slots)
    place_ids = lax.broadcasted_iota(jnp.int32, (slots, places), 1)
    onehot = (flat_ids[:, None] == place_ids).astype(jnp.float32)
    placed = jnp.einsum("np,ncs->pcs", onehot, flat_sums, precision=lax.Precision.HIGHEST)
    surface = (
        placed.reshape(places_x, northing_places, 3, PATCH_X, PATCH_Y)
        .transpose(2, 0, 3, 1, 4)
        .reshape(3, local_x, local_y)
    )
    surface = lax.psum(surface, "gz")
    source = scale * depth_kernel[None, :, None, None] * surface[:, None, :, :]
    adjoint_field = jnp.zeros_like(source)
    cg_residual = source
    image = operate(cg_residual, stiffness)
    norm_now, product = two_products(cg_residual, image)
    alpha = norm_now / product
    direction = cg_residual
    along = image
    for step in range(ITERS):
        adjoint_field = adjoint_field + alpha * direction
        cg_residual = cg_residual - alpha * along
        if step + 1 < ITERS:
            image = operate(cg_residual, stiffness)
            norm_next, product = two_products(cg_residual, image)
            ratio = norm_next / norm_now
            alpha = norm_next / (product - ratio * norm_next / alpha)
            direction = cg_residual + ratio * direction
            along = image + ratio * along
            norm_now = norm_next
    return (adjoint_field, cg_residual)


def solution(mesh):
    in_specs = (
        P(("grp", "gx", "gy", "gz"), None, None),
        P(("grp", "gx", "gy", "gz"), None, None),
        P(("grp", "gx", "gy", "gz"), None),
        P(("grp", "gx", "gy", "gz")),
        P(("grp", "gx", "gy", "gz"), None),
        P(("grp", "gx", "gy", "gz")),
        P(("grp", "gx", "gy", "gz")),
        P(),
        P(),
        P(("grp", "gz")),
        P(("grp", "gz"), "gx", "gy"),
    )
    out_specs = (P(None, ("grp", "gz"), "gx", "gy"), P(None, ("grp", "gz"), "gx", "gy"))
    return jax.shard_map(
        per_device, mesh=mesh, in_specs=in_specs, out_specs=out_specs, check_vma=False
    )
```

profile of v0, /device:TPU:0, one launch (start us, length us, event | category | flops | bytes accessed | tf_op | source)
XLA Modules:
  0.0 349.5 jit_solution(3229247939557360916)
XLA Ops:
  3.7 7.3 %all-to-all-start.2 = ((s32[8,1,16]{2,1,0:T(1,128)}), s32[8,1,16]{2,1,0:T(1,128)S(1)}, u32[]{:S(2)}, u32[]{:S(2)}) async-start(s32[8,1,16]{2,1,0:T(1,128)} %bitcast.17), calls=%async_computation.2 | async-start | bytes 8192 | tf_op jit(solution)/shard_map/all_to_all | solution.py:142
  11.0 1.5 fusion.98
  12.5 1.8 multiply_reduce_fusion.4
  15.0 2.4 all-to-all-done.2
  17.4 3.6 %all-to-all-start = ((s32[8,1,16]{2,1,0:T(1,128)}), s32[8,1,16]{2,1,0:T(1,128)S(1)}, u32[]{:S(2)}, u32[]{:S(2)}) async-start(s32[8,1,16]{2,1,0:T(1,128)} %bitcast.8), calls=%async_computation | async-start | bytes 8192 | tf_op jit(solution)/shard_map/all_to_all | solution.py:143
  22.4 5.1 %all-to-all-done = s32[8,1,16]{2,1,0:T(1,128)S(1)} async-done(((s32[8,1,16]{2,1,0:T(1,128)}), s32[8,1,16]{2,1,0:T(1,128)S(1)}, u32[]{:S(2)}, u32[]{:S(2)}) %all-to-all-start) | async-done | bytes 544 | tf_op jit(solution)/shard_map/all_to_all | solution.py:143
  27.4 3.5 %all-to-all-start.1 = ((f32[8,16,4,256]{3,1,2,0:T(8,128)}), f32[8,16,4,256]{3,1,2,0:T(8,128)S(1)}, u32[]{:S(2)}, u32[]{:S(2)}) async-start(f32[8,16,4,256]{3,1,2,0:T(8,128)} %copy.111), calls=%async_computation.1 | async-start | bytes 1048576 | tf_op jit(solution)/shard_map/all_to_all | solution.py:141
  31.0 34.7 %all-reduce.3 = (f32[]{:T(128)}, f32[]{:T(128)}) all-reduce(f32[]{:T(128)} %get-tuple-element.64, f32[]{:T(128)} %get-tuple-element.62), channel_id=1, replica_groups=mesh['grp'=2,'gx'=4,'gy'=2,'gz'=2] {'gx','gy','gz'}, use_global_device_ids=true, to_apply=%region_1.0 | all-reduce | flops 2 | bytes 16 | tf_op jit(solution)/shard_map/psum | solution.py:121
  70.3 17.3 %while.10 = (s32[]{:T(128)}, f32[4,32,3,128]{3,2,1,0:T(4,128)S(1)}, bf16[4,32,3,256]{3,2,1,0:T(4,128)(2,1)S(1)}, s32[4,32]{1,0:T(4,128)S(1)}, bf16[32,256,128]{2,1,0:T(8,128)(2,1)S(1)}, /*index=5*/s32[]{:T(128)}) while((s32[]{:T(128)}, f32[4,32,3,128]{3,2,1,0:T(4,128)S(1)}, bf16[4,32,3,256]{3,2,1,0:T(4,128)(2,1)S(1)}, s32[4,32]{1,0:T(4,128)S(1)}, ...), condition=%wide.region_8.9_spmd, body=%wide.region_7.8_spmd.sunk | while | flops 7341346 | bytes 6428917 | solution.py:86
  70.4 2.2 gather_fusion
  72.6 2.1 fusion.120
  74.7 2.2 gather_fusion
  76.9 2.1 fusion.120
  79.0 2.2 gather_fusion
  81.2 2.1 fusion.120
  83.3 2.2 gather_fusion
  85.5 2.1 fusion.120
  88.9 3.5 %psum.65 = f32[3,32,128]{2,1,0:T(8,128)S(1)} all-reduce(f32[3,32,128]{2,1,0:T(8,128)S(1)} %reshape.93), channel_id=1, replica_groups=mesh['grp'=2,'gx'=4,'gy'=2,'gz'=2] {'gz'}, use_global_device_ids=true, to_apply=%region_9.10 | all-reduce | flops 12288 | bytes 98304 | tf_op jit(solution)/shard_map/psum | solution.py:159
  93.9 1.3 collective-permute-start.1
  95.4 4.2 %collective-permute-done.1 = f32[3,16,1,128]{3,1,2,0:T(8,128)S(1)} collective-permute-done((f32[3,16,1,128]{3,1,2,0:T(8,128)S(1)}, f32[3,16,1,128]{3,1,2,0:T(8,128)S(1)}, u32[]{:S(2)}, u32[]{:S(2)}) %collective-permute-start.1) | collective-permute-done | bytes 24608 | tf_op jit(solution)/shard_map/ppermute | solution.py:26
  104.0 3.9 %collective-permute-done.3 = f32[3,16,34,1]{2,1,3,0:T(8,128)S(1)} collective-permute-done((f32[3,16,34,1]{2,1,3,0:T(8,128)S(1)}, f32[3,16,34,1]{2,1,3,0:T(8,128)S(1)}, u32[]{:S(2)}, u32[]{:S(2)}) %collective-permute-start.3) | collective-permute-done | bytes 6560 | tf_op jit(solution)/shard_map/ppermute | solution.py:26
  109.1 1.3 collective-permute-start.4
  110.4 1.3 collective-permute-start.5
  111.7 1.9 collective-permute-done.5
  115.4 2.5 collective-permute-start.7
  117.9 1.3 collective-permute-start.6
  119.3 4.2 %collective-permute-done.6 = f32[16,1,128]{2,0,1:T(8,128)S(1)} collective-permute-done((f32[16,1,128]{2,0,1:T(8,128)S(1)}, f32[16,1,128]{2,0,1:T(8,128)S(1)}, u32[]{:S(2)}, u32[]{:S(2)}) %collective-permute-start.6) | collective-permute-done | bytes 8224 | tf_op jit(solution)/shard_map/ppermute | solution.py:26
  123.6 1.6 collective-permute-start.9
  125.3 1.3 collective-permute-start.8
  127.1 3.3 collective-permute-done.9
  130.3 4.1 %collective-permute-done.8 = f32[16,34,1]{2,0,1:T(8,128)S(1)} collective-permute-done((f32[16,34,1]{2,0,1:T(8,128)S(1)}, f32[16,34,1]{2,0,1:T(8,128)S(1)}, u32[]{:S(2)}, u32[]{:S(2)}) %collective-permute-start.8) | collective-permute-done | bytes 2208 | tf_op jit(solution)/shard_map/ppermute | solution.py:26
  134.8 1.3 collective-permute-start.10
  136.1 3.3 collective-permute-start.11
  141.7 30.5 %all-reduce.2 = (f32[]{:T(128)}, f32[]{:T(128)}) all-reduce(f32[]{:T(128)} %get-tuple-element.41, f32[]{:T(128)} %get-tuple-element.40), channel_id=1, replica_groups=mesh['grp'=2,'gx'=4,'gy'=2,'gz'=2] {'gx','gy','gz'}, use_global_device_ids=true, to_apply=%region_11.12 | all-reduce | flops 2 | bytes 16 | tf_op jit(solution)/shard_map/psum | solution.py:91
  175.0 1.3 collective-permute-start.13
  176.5 4.2 %collective-permute-done.13 = f32[3,16,1,128]{3,1,2,0:T(8,128)S(1)} collective-permute-done((f32[3,16,1,128]{3,1,2,0:T(8,128)S(1)}, f32[3,16,1,128]{3,1,2,0:T(8,128)S(1)}, u32[]{:S(2)}, u32[]{:S(2)}) %collective-permute-start.13) | collective-permute-done | bytes 24608 | tf_op jit(solution)/shard_map/ppermute | solution.py:26
  186.3 4.0 %collective-permute-done.15 = f32[3,16,34,1]{2,1,3,0:T(8,128)} collective-permute-done((f32[3,16,34,1]{2,1,3,0:T(8,128)S(1)}, f32[3,16,34,1]{2,1,3,0:T(8,128)}, u32[]{:S(2)}, u32[]{:S(2)}) %collective-permute-start.15) | collective-permute-done | bytes 6560 | tf_op jit(solution)/shard_map/ppermute | solution.py:26
  191.6 1.5 pad_maximum_fusion.75
  193.1 1.3 collective-permute-start.16
  194.4 1.3 collective-permute-start.17
  195.7 1.9 collective-permute-done.17
  199.4 2.0 collective-permute-start.19
  201.4 1.3 collective-permute-start.18
  202.7 4.2 %collective-permute-done.18 = f32[16,1,128]{2,0,1:T(8,128)S(1)} collective-permute-done((f32[16,1,128]{2,0,1:T(8,128)S(1)}, f32[16,1,128]{2,0,1:T(8,128)S(1)}, u32[]{:S(2)}, u32[]{:S(2)}) %collective-permute-start.18) | collective-permute-done | bytes 8224 | tf_op jit(solution)/shard_map/ppermute | solution.py:26
  207.1 1.5 collective-permute-start.21
  210.4 3.1 collective-permute-done.21
  213.5 4.1 %collective-permute-done.20 = f32[16,34,1]{2,0,1:T(8,128)S(1)} collective-permute-done((f32[16,34,1]{2,0,1:T(8,128)S(1)}, f32[16,34,1]{2,0,1:T(8,128)S(1)}, u32[]{:S(2)}, u32[]{:S(2)}) %collective-permute-start.20) | collective-permute-done | bytes 2208 | tf_op jit(solution)/shard_map/ppermute | solution.py:26
  219.3 3.2 collective-permute-start.23
  225.0 30.5 %all-reduce.1 = (f32[]{:T(128)}, f32[]{:T(128)}) all-reduce(f32[]{:T(128)} %get-tuple-element.39, f32[]{:T(128)} %get-tuple-element.38), channel_id=1, replica_groups=mesh['grp'=2,'gx'=4,'gy'=2,'gz'=2] {'gx','gy','gz'}, use_global_device_ids=true, to_apply=%region_15.16 | all-reduce | flops 2 | bytes 16 | tf_op jit(solution)/shard_map/psum | solution.py:91
  263.0 4.2 %collective-permute-done.25 = f32[3,16,1,128]{3,1,2,0:T(8,128)S(1)} collective-permute-done((f32[3,16,1,128]{3,1,2,0:T(8,128)S(1)}, f32[3,16,1,128]{3,1,2,0:T(8,128)S(1)}, u32[]{:S(2)}, u32[]{:S(2)}) %collective-permute-start.25) | collective-permute-done | bytes 24608 | tf_op jit(solution)/shard_map/ppermute | solution.py:26
  268.5 1.6 copy.139
  271.8 1.5 collective-permute-start.27
  273.8 3.8 %collective-permute-done.27 = f32[3,16,34,1]{2,1,3,0:T(8,128)} collective-permute-done((f32[3,16,34,1]{2,1,3,0:T(8,128)S(1)}, f32[3,16,34,1]{2,1,3,0:T(8,128)}, u32[]{:S(2)}, u32[]{:S(2)}) %collective-permute-start.27) | collective-permute-done | bytes 6560 | tf_op jit(solution)/shard_map/ppermute | solution.py:26
  278.9 1.5 pad_maximum_fusion.70
  280.4 1.3 collective-permute-start.28
  283.0 1.9 collective-permute-done.29
  286.7 2.0 collective-permute-start.31
  288.7 1.3 collective-permute-start.30
  290.0 4.2 %collective-permute-done.30 = f32[16,1,128]{2,0,1:T(8,128)S(1)} collective-permute-done((f32[16,1,128]{2,0,1:T(8,128)S(1)}, f32[16,1,128]{2,0,1:T(8,128)S(1)}, u32[]{:S(2)}, u32[]{:S(2)}) %collective-permute-start.30) | collective-permute-done | bytes 8224 | tf_op jit(solution)/shard_map/ppermute | solution.py:26
  294.4 1.5 collective-permute-start.33
  297.7 3.1 collective-permute-done.33
  300.8 4.1 %collective-permute-done.32 = f32[16,34,1]{2,0,1:T(8,128)S(1)} collective-permute-done((f32[16,34,1]{2,0,1:T(8,128)S(1)}, f32[16,34,1]{2,0,1:T(8,128)S(1)}, u32[]{:S(2)}, u32[]{:S(2)}) %collective-permute-start.32) | collective-permute-done | bytes 2208 | tf_op jit(solution)/shard_map/ppermute | solution.py:26
  306.6 3.2 collective-permute-start.35
  312.4 30.4 %all-reduce = (f32[]{:T(128)}, f32[]{:T(128)}) all-reduce(f32[]{:T(128)} %get-tuple-element.37, f32[]{:T(128)} %get-tuple-element.36), channel_id=1, replica_groups=mesh['grp'=2,'gx'=4,'gy'=2,'gz'=2] {'gx','gy','gz'}, use_global_device_ids=true, to_apply=%region_19.20 | all-reduce | flops 2 | bytes 16 | tf_op jit(solution)/shard_map/psum | solution.py:91
  (162 shorter events, 58.1 us)
Async XLA Ops:
  0.6 68.6 %copy-start = (f32[4,3]{1,0:T(4,128)S(1)}, f32[4,3]{1,0:T(4,128)}, u32[]{:S(2)}) copy-start(f32[4,3]{1,0:T(4,128)} %param.20) | copy-start | bytes 148
  0.6 66.3 %copy-start.17 = (f32[16]{0:T(128)S(1)}, f32[16]{0:T(128)}, u32[]{:S(2)}) copy-start(f32[16]{0:T(128)} %param.22) | copy-start | bytes 196
  3.7 13.7 %all-to-all-start.2 = ((s32[8,1,16]{2,1,0:T(1,128)}), s32[8,1,16]{2,1,0:T(1,128)S(1)}, u32[]{:S(2)}, u32[]{:S(2)}) async-start(s32[8,1,16]{2,1,0:T(1,128)} %bitcast.17), calls=%async_computation.2 | async-start | bytes 8192 | tf_op jit(solution)/shard_map/all_to_all | solution.py:142
  14.4 56.0 %copy-start.1 = (bf16[32,256,128]{2,1,0:T(8,128)(2,1)S(1)}, bf16[32,256,128]{2,1,0:T(8,128)(2,1)}, u32[]{:S(2)}) copy-start(bf16[32,256,128]{2,1,0:T(8,128)(2,1)} %param.21) | copy-start | bytes 6291460
  17.4 10.1 %all-to-all-start = ((s32[8,1,16]{2,1,0:T(1,128)}), s32[8,1,16]{2,1,0:T(1,128)S(1)}, u32[]{:S(2)}, u32[]{:S(2)}) async-start(s32[8,1,16]{2,1,0:T(1,128)} %bitcast.8), calls=%async_computation | async-start | bytes 8192 | tf_op jit(solution)/shard_map/all_to_all | solution.py:143
  27.4 41.5 %all-to-all-start.1 = ((f32[8,16,4,256]{3,1,2,0:T(8,128)}), f32[8,16,4,256]{3,1,2,0:T(8,128)S(1)}, u32[]{:S(2)}, u32[]{:S(2)}) async-start(f32[8,16,4,256]{3,1,2,0:T(8,128)} %copy.111), calls=%async_computation.1 | async-start | bytes 1048576 | tf_op jit(solution)/shard_map/all_to_all | solution.py:141
  92.4 7.5 %copy-start.9 = (f32[3,32,128]{2,1,0:T(8,128)}, f32[3,32,128]{2,1,0:T(8,128)S(1)}, u32[]{:S(2)}) copy-start(f32[3,32,128]{2,1,0:T(8,128)S(1)} %psum.65) | copy-start | bytes 147460
  92.6 2.8 collective-permute-start
  93.9 5.7 %collective-permute-start.1 = (f32[3,16,1,128]{3,1,2,0:T(8,128)S(1)}, f32[3,16,1,128]{3,1,2,0:T(8,128)S(1)}, u32[]{:S(2)}, u32[]{:S(2)}) collective-permute-start(f32[3,16,1,128]{3,1,2,0:T(8,128)S(1)} %get-tuple-element.100), channel_id=1, source_target_pairs={{4,0},{8,4},{12,8},{5,1},{9,5},{13,9},{6,2},{10,6},{14,10},{7,3},{... | collective-permute-start | bytes 73736 | tf_op jit(solution)/shard_map/ppermute | solution.py:26
  100.4 3.1 collective-permute-start.2
  102.2 5.7 %collective-permute-start.3 = (f32[3,16,34,1]{2,1,3,0:T(8,128)S(1)}, f32[3,16,34,1]{2,1,3,0:T(8,128)S(1)}, u32[]{:S(2)}, u32[]{:S(2)}) collective-permute-start(f32[3,16,34,1]{2,1,3,0:T(8,128)S(1)} %copy.136), channel_id=1, source_target_pairs={{2,0},{3,1},{6,4},{7,5},{10,8},{11,9},{14,12},{15,13},{18,16},{19,... | collective-permute-start | bytes 19592 | tf_op jit(solution)/shard_map/ppermute | solution.py:26
  109.1 2.6 collective-permute-start.4
  110.4 3.2 collective-permute-start.5
  115.0 11.6 %copy-start.2 = (f32[16,32,128]{2,1,0:T(8,128)S(1)}, f32[16,32,128]{2,1,0:T(8,128)}, u32[]{:S(2)}) copy-start(f32[16,32,128]{2,1,0:T(8,128)} %param.23) | copy-start | bytes 786436
  115.4 3.8 %collective-permute-start.7 = (f32[16,1,128]{2,0,1:T(8,128)S(1)}, f32[16,1,128]{2,0,1:T(8,128)S(1)}, u32[]{:S(2)}, u32[]{:S(2)}) collective-permute-start(f32[16,1,128]{2,0,1:T(8,128)S(1)} %get-tuple-element.111), channel_id=1, source_target_pairs={{0,4},{4,8},{8,12},{1,5},{5,9},{9,13},{2,6},{6,10},{10,14},{3,7},{... | collective-permute-start | bytes 24584 | tf_op jit(solution)/shard_map/ppermute | solution.py:24
  117.9 5.5 %collective-permute-start.6 = (f32[16,1,128]{2,0,1:T(8,128)S(1)}, f32[16,1,128]{2,0,1:T(8,128)S(1)}, u32[]{:S(2)}, u32[]{:S(2)}) collective-permute-start(f32[16,1,128]{2,0,1:T(8,128)S(1)} %get-tuple-element.112), channel_id=1, source_target_pairs={{4,0},{8,4},{12,8},{5,1},{9,5},{13,9},{6,2},{10,6},{14,10},{7,3},{... | collective-permute-start | bytes 24584 | tf_op jit(solution)/shard_map/ppermute | solution.py:26
  123.6 6.7 %collective-permute-start.9 = (f32[16,34,1]{2,0,1:T(8,128)S(1)}, f32[16,34,1]{2,0,1:T(8,128)S(1)}, u32[]{:S(2)}, u32[]{:S(2)}) collective-permute-start(f32[16,34,1]{2,0,1:T(8,128)S(1)} %get-tuple-element.105), channel_id=1, source_target_pairs={{0,2},{1,3},{4,6},{5,7},{8,10},{9,11},{12,14},{13,15},{16,18},{17,... | collective-permute-start | bytes 6536 | tf_op jit(solution)/shard_map/ppermute | solution.py:24
  125.3 9.2 %collective-permute-start.8 = (f32[16,34,1]{2,0,1:T(8,128)S(1)}, f32[16,34,1]{2,0,1:T(8,128)S(1)}, u32[]{:S(2)}, u32[]{:S(2)}) collective-permute-start(f32[16,34,1]{2,0,1:T(8,128)S(1)} %get-tuple-element.106), channel_id=1, source_target_pairs={{2,0},{3,1},{6,4},{7,5},{10,8},{11,9},{14,12},{15,13},{18,16},{19,... | collective-permute-start | bytes 6536 | tf_op jit(solution)/shard_map/ppermute | solution.py:26
  134.8 5.3 %collective-permute-start.10 = (f32[1,34,130]{2,0,1:T(1,128)S(1)}, f32[1,34,130]{2,0,1:T(1,128)S(1)}, u32[]{:S(2)}, u32[]{:S(2)}) collective-permute-start(f32[1,34,130]{2,0,1:T(1,128)S(1)} %get-tuple-element.89), channel_id=1, source_target_pairs={{1,0},{3,2},{5,4},{7,6},{9,8},{11,10},{13,12},{15,14},{17,16},{19,... | collective-permute-start | bytes 53048 | tf_op jit(solution)/shard_map/ppermute | solution.py:26
  136.1 4.7 %copy-start.10 = (f32[3,32,128]{2,1,0:T(8,128)S(1)}, f32[3,32,128]{2,1,0:T(8,128)}, u32[]{:S(2)}) copy-start(f32[3,32,128]{2,1,0:T(8,128)} %copy-done.9) | copy-start | bytes 147460
  136.1 4.0 %collective-permute-start.11 = (f32[1,34,130]{2,0,1:T(1,128)S(1)}, f32[1,34,130]{2,0,1:T(1,128)S(1)}, u32[]{:S(2)}, u32[]{:S(2)}) collective-permute-start(f32[1,34,130]{2,0,1:T(1,128)S(1)} %get-tuple-element.90), channel_id=1, source_target_pairs={{0,1},{2,3},{4,5},{6,7},{8,9},{10,11},{12,13},{14,15},{16,17},{18,... | collective-permute-start | bytes 53048 | tf_op jit(solution)/shard_map/ppermute | solution.py:24
  173.7 2.8 collective-permute-start.12
  175.0 5.7 %collective-permute-start.13 = (f32[3,16,1,128]{3,1,2,0:T(8,128)S(1)}, f32[3,16,1,128]{3,1,2,0:T(8,128)S(1)}, u32[]{:S(2)}, u32[]{:S(2)}) collective-permute-start(f32[3,16,1,128]{3,1,2,0:T(8,128)S(1)} %get-tuple-element.98), channel_id=1, source_target_pairs={{4,0},{8,4},{12,8},{5,1},{9,5},{13,9},{6,2},{10,6},{14,10},{7,3},{... | collective-permute-start | bytes 73736 | tf_op jit(solution)/shard_map/ppermute | solution.py:26
  180.7 0.6 copy-start.13
  182.8 3.0 collective-permute-start.14
  184.5 5.8 %collective-permute-start.15 = (f32[3,16,34,1]{2,1,3,0:T(8,128)S(1)}, f32[3,16,34,1]{2,1,3,0:T(8,128)}, u32[]{:S(2)}, u32[]{:S(2)}) collective-permute-start(f32[3,16,34,1]{2,1,3,0:T(8,128)S(1)} %copy.138), channel_id=1, source_target_pairs={{2,0},{3,1},{6,4},{7,5},{10,8},{11,9},{14,12},{15,13},{18,16},{19,... | collective-permute-start | bytes 19592 | tf_op jit(solution)/shard_map/ppermute | solution.py:26
  191.6 6.0 %copy-start.14 = (f32[3,16,1,128]{3,1,2,0:T(8,128)S(1)}, f32[3,16,1,128]{3,1,2,0:T(8,128)}, u32[]{:S(2)}) copy-start(f32[3,16,1,128]{3,1,2,0:T(8,128)} %copy-done.13) | copy-start | bytes 73732
  193.1 2.6 collective-permute-start.16
  194.4 3.2 collective-permute-start.17
  199.4 3.3 collective-permute-start.19
  201.4 5.5 %collective-permute-start.18 = (f32[16,1,128]{2,0,1:T(8,128)S(1)}, f32[16,1,128]{2,0,1:T(8,128)S(1)}, u32[]{:S(2)}, u32[]{:S(2)}) collective-permute-start(f32[16,1,128]{2,0,1:T(8,128)S(1)} %get-tuple-element.110), channel_id=1, source_target_pairs={{4,0},{8,4},{12,8},{5,1},{9,5},{13,9},{6,2},{10,6},{14,10},{7,3},{... | collective-permute-start | bytes 24584 | tf_op jit(solution)/shard_map/ppermute | solution.py:26
  207.1 6.5 %collective-permute-start.21 = (f32[16,34,1]{2,0,1:T(8,128)S(1)}, f32[16,34,1]{2,0,1:T(8,128)S(1)}, u32[]{:S(2)}, u32[]{:S(2)}) collective-permute-start(f32[16,34,1]{2,0,1:T(8,128)S(1)} %get-tuple-element.103), channel_id=1, source_target_pairs={{0,2},{1,3},{4,6},{5,7},{8,10},{9,11},{12,14},{13,15},{16,18},{17,... | collective-permute-start | bytes 6536 | tf_op jit(solution)/shard_map/ppermute | solution.py:24
  208.6 9.0 %collective-permute-start.20 = (f32[16,34,1]{2,0,1:T(8,128)S(1)}, f32[16,34,1]{2,0,1:T(8,128)S(1)}, u32[]{:S(2)}, u32[]{:S(2)}) collective-permute-start(f32[16,34,1]{2,0,1:T(8,128)S(1)} %get-tuple-element.104), channel_id=1, source_target_pairs={{2,0},{3,1},{6,4},{7,5},{10,8},{11,9},{14,12},{15,13},{18,16},{19,... | collective-permute-start | bytes 6536 | tf_op jit(solution)/shard_map/ppermute | solution.py:26
  210.4 49.5 %copy-start.3 = (f32[1,16,32,128]{3,1,2,0:T(8,128)}, f32[1,16,32,128]{3,1,2,0:T(8,128)S(1)}, u32[]{:S(2)}) copy-start(f32[1,16,32,128]{3,1,2,0:T(8,128)S(1)} %fusion.59) | copy-start | bytes 786436
  218.0 5.1 %collective-permute-start.22 = (f32[1,34,130]{2,0,1:T(1,128)S(1)}, f32[1,34,130]{2,0,1:T(1,128)S(1)}, u32[]{:S(2)}, u32[]{:S(2)}) collective-permute-start(f32[1,34,130]{2,0,1:T(1,128)S(1)} %get-tuple-element.85), channel_id=1, source_target_pairs={{1,0},{3,2},{5,4},{7,6},{9,8},{11,10},{13,12},{15,14},{17,16},{19,... | collective-permute-start | bytes 53048 | tf_op jit(solution)/shard_map/ppermute | solution.py:26
  219.3 4.7 %copy-start.11 = (f32[3,32,128]{2,1,0:T(8,128)S(1)}, f32[3,32,128]{2,1,0:T(8,128)}, u32[]{:S(2)}) copy-start(f32[3,32,128]{2,1,0:T(8,128)} %copy-done.9) | copy-start | bytes 147460
  219.3 4.0 %collective-permute-start.23 = (f32[1,34,130]{2,0,1:T(1,128)S(1)}, f32[1,34,130]{2,0,1:T(1,128)S(1)}, u32[]{:S(2)}, u32[]{:S(2)}) collective-permute-start(f32[1,34,130]{2,0,1:T(1,128)S(1)} %get-tuple-element.86), channel_id=1, source_target_pairs={{0,1},{2,3},{4,5},{6,7},{8,9},{10,11},{12,13},{14,15},{16,17},{18,... | collective-permute-start | bytes 53048 | tf_op jit(solution)/shard_map/ppermute | solution.py:24
  223.1 37.0 %copy-start.5 = (f32[1,16,32,128]{3,1,2,0:T(8,128)}, f32[1,16,32,128]{3,1,2,0:T(8,128)S(1)}, u32[]{:S(2)}) copy-start(f32[1,16,32,128]{3,1,2,0:T(8,128)S(1)} %fusion.51) | copy-start | bytes 786436
  224.0 43.3 %copy-start.7 = (f32[1,16,32,128]{3,1,2,0:T(8,128)}, f32[1,16,32,128]{3,1,2,0:T(8,128)S(1)}, u32[]{:S(2)}) copy-start(f32[1,16,32,128]{3,1,2,0:T(8,128)S(1)} %fusion.45) | copy-start | bytes 786436
  260.2 2.8 collective-permute-start.24
  261.5 5.7 %collective-permute-start.25 = (f32[3,16,1,128]{3,1,2,0:T(8,128)S(1)}, f32[3,16,1,128]{3,1,2,0:T(8,128)S(1)}, u32[]{:S(2)}, u32[]{:S(2)}) collective-permute-start(f32[3,16,1,128]{3,1,2,0:T(8,128)S(1)} %get-tuple-element.96), channel_id=1, source_target_pairs={{4,0},{8,4},{12,8},{5,1},{9,5},{13,9},{6,2},{10,6},{14,10},{7,3},{... | collective-permute-start | bytes 73736 | tf_op jit(solution)/shard_map/ppermute | solution.py:26
  267.2 1.3 copy-start.15
  270.0 3.3 collective-permute-start.26
  271.8 5.8 %collective-permute-start.27 = (f32[3,16,34,1]{2,1,3,0:T(8,128)S(1)}, f32[3,16,34,1]{2,1,3,0:T(8,128)}, u32[]{:S(2)}, u32[]{:S(2)}) collective-permute-start(f32[3,16,34,1]{2,1,3,0:T(8,128)S(1)} %copy.140), channel_id=1, source_target_pairs={{2,0},{3,1},{6,4},{7,5},{10,8},{11,9},{14,12},{15,13},{18,16},{19,... | collective-permute-start | bytes 19592 | tf_op jit(solution)/shard_map/ppermute | solution.py:26
  278.9 6.0 %copy-start.16 = (f32[3,16,1,128]{3,1,2,0:T(8,128)S(1)}, f32[3,16,1,128]{3,1,2,0:T(8,128)}, u32[]{:S(2)}) copy-start(f32[3,16,1,128]{3,1,2,0:T(8,128)} %copy-done.15) | copy-start | bytes 73732
  280.4 2.6 collective-permute-start.28
  281.7 3.2 collective-permute-start.29
  286.7 3.3 collective-permute-start.31
  288.7 5.5 %collective-permute-start.30 = (f32[16,1,128]{2,0,1:T(8,128)S(1)}, f32[16,1,128]{2,0,1:T(8,128)S(1)}, u32[]{:S(2)}, u32[]{:S(2)}) collective-permute-start(f32[16,1,128]{2,0,1:T(8,128)S(1)} %get-tuple-element.108), channel_id=1, source_target_pairs={{4,0},{8,4},{12,8},{5,1},{9,5},{13,9},{6,2},{10,6},{14,10},{7,3},{... | collective-permute-start | bytes 24584 | tf_op jit(solution)/shard_map/ppermute | solution.py:26
  294.4 6.4 %collective-permute-start.33 = (f32[16,34,1]{2,0,1:T(8,128)S(1)}, f32[16,34,1]{2,0,1:T(8,128)S(1)}, u32[]{:S(2)}, u32[]{:S(2)}) collective-permute-start(f32[16,34,1]{2,0,1:T(8,128)S(1)} %get-tuple-element.101), channel_id=1, source_target_pairs={{0,2},{1,3},{4,6},{5,7},{8,10},{9,11},{12,14},{13,15},{16,18},{17,... | collective-permute-start | bytes 6536 | tf_op jit(solution)/shard_map/ppermute | solution.py:24
  295.9 9.0 %collective-permute-start.32 = (f32[16,34,1]{2,0,1:T(8,128)S(1)}, f32[16,34,1]{2,0,1:T(8,128)S(1)}, u32[]{:S(2)}, u32[]{:S(2)}) collective-permute-start(f32[16,34,1]{2,0,1:T(8,128)S(1)} %get-tuple-element.102), channel_id=1, source_target_pairs={{2,0},{3,1},{6,4},{7,5},{10,8},{11,9},{14,12},{15,13},{18,16},{19,... | collective-permute-start | bytes 6536 | tf_op jit(solution)/shard_map/ppermute | solution.py:26
  305.2 5.2 %collective-permute-start.34 = (f32[1,34,130]{2,0,1:T(1,128)S(1)}, f32[1,34,130]{2,0,1:T(1,128)S(1)}, u32[]{:S(2)}, u32[]{:S(2)}) collective-permute-start(f32[1,34,130]{2,0,1:T(1,128)S(1)} %get-tuple-element.81), channel_id=1, source_target_pairs={{1,0},{3,2},{5,4},{7,6},{9,8},{11,10},{13,12},{15,14},{17,16},{19,... | collective-permute-start | bytes 53048 | tf_op jit(solution)/shard_map/ppermute | solution.py:26
  306.5 4.7 %copy-start.4 = (f32[1,16,32,128]{3,1,2,0:T(8,128)S(1)}, f32[1,16,32,128]{3,1,2,0:T(8,128)}, u32[]{:S(2)}) copy-start(f32[1,16,32,128]{3,1,2,0:T(8,128)} %copy-done.3) | copy-start | bytes 786436
  306.5 4.7 %copy-start.6 = (f32[1,16,32,128]{3,1,2,0:T(8,128)S(1)}, f32[1,16,32,128]{3,1,2,0:T(8,128)}, u32[]{:S(2)}) copy-start(f32[1,16,32,128]{3,1,2,0:T(8,128)} %copy-done.5) | copy-start | bytes 786436
  306.5 4.7 %copy-start.8 = (f32[1,16,32,128]{3,1,2,0:T(8,128)S(1)}, f32[1,16,32,128]{3,1,2,0:T(8,128)}, u32[]{:S(2)}) copy-start(f32[1,16,32,128]{3,1,2,0:T(8,128)} %copy-done.7) | copy-start | bytes 786436
  306.6 4.7 %copy-start.12 = (f32[3,32,128]{2,1,0:T(8,128)S(1)}, f32[3,32,128]{2,1,0:T(8,128)}, u32[]{:S(2)}) copy-start(f32[3,32,128]{2,1,0:T(8,128)} %copy-done.9) | copy-start | bytes 147460
  306.6 4.0 %collective-permute-start.35 = (f32[1,34,130]{2,0,1:T(1,128)S(1)}, f32[1,34,130]{2,0,1:T(1,128)S(1)}, u32[]{:S(2)}, u32[]{:S(2)}) collective-permute-start(f32[1,34,130]{2,0,1:T(1,128)S(1)} %get-tuple-element.82), channel_id=1, source_target_pairs={{0,1},{2,3},{4,5},{6,7},{8,9},{10,11},{12,13},{14,15},{16,17},{18,... | collective-permute-start | bytes 53048 | tf_op jit(solution)/shard_map/ppermute | solution.py:24
where the time goes:
time: 351 us; the launch traced here: 349 us
  blocking collectives  130 us (37%)
  waiting for transfers between devices  73.2 us (21%)
  starting transfers between devices  70.3 us (20%)
  local copies, waits for them, and re-layouts  26.9 us (8%)
  other arithmetic  26.2 us (7%)
  between operations  12.4 us (4%)
  matrix products  10.8 us (3%)
    psum x3, blocking collectives, two_products(): lax.psum((jnp.sum(residual * residual), jnp.sum(residual * image)), ('gx'...  91.4 us
    ppermute x18, waiting for transfers between devices, extended(): lax.ppermute(head, axis, [((i + 1) % count, i) for i in range(ends)])  55 us
    psum x1, blocking collectives, per_device(): lax.psum((jnp.sum(resid * resid), jnp.sum(valid)), ('gx', 'gy', 'gz'))  34.7 us
    ppermute x18, starting transfers between devices, extended(): lax.ppermute(tail, axis, [(i, (i + 1) % count) for i in range(ends)])  32.4 us
    ppermute x18, starting transfers between devices, extended(): lax.ppermute(head, axis, [((i + 1) % count, i) for i in range(ends)])  23.5 us
    ppermute x18, waiting for transfers between devices, extended(): lax.ppermute(tail, axis, [(i, (i + 1) % count) for i in range(ends)])  10.7 us
    gather x4, local copies, waits for them, and re-layouts, per_group(): selected_entries = jnp.take(weights, block_tables, axis=0)  8.72 us
    dot_general x4, matrix products, per_group(): jnp.einsum('aow,awv->aov', block_coefficient_values, selected_entries, pr...  8.3 us
  transfers between devices with their start and end apart: 39, of which 25 were waited for; matrix products, arithmetic and copies ran while one was open for 4% of the time, Pallas kernels for 0%

commit v1 on v0

--- a/solution.py
+++ b/solution.py
@@ -1,3 +1,4 @@
+import functools
 import math
 import jax
 import jax.numpy as jnp
@@ -11,6 +12,14 @@
 KAPPA = 0.5
 EPS = 1e-06
 SPATIAL = (1, 2, 0)
+
+
+def group_the_region(m, mesh_name, chip_axis):
+    back = lax.psum(m, mesh_name)
+    return lax.psum(back, chip_axis)
+
+
+number_lots_all = functools.partial(group_the_region, mesh_name=("gy", "gz"), chip_axis="gx")
 
 
 def extended(cells, sides, width):
@@ -118,7 +127,7 @@
     column = lax.broadcasted_iota(jnp.int32, (blocks, pixels), 1)
     valid = coherence_mask.astype(jnp.float32) * (column < block_count[:, None]).astype(jnp.float32)
     resid = (predicted - observed) * valid[:, None, :]
-    misfit, weight = lax.psum((jnp.sum(resid * resid), jnp.sum(valid)), ("gx", "gy", "gz"))
+    misfit, weight = number_lots_all((jnp.sum(resid * resid), jnp.sum(valid)))
     scale = lax.rsqrt(misfit / (EPOCHS * weight) + EPS)
     owner = block_owner[:, 0]
     order = lax.broadcasted_iota(jnp.int32, (blocks, blocks), 0)

time: 351 us -> 339 us (0.966)
  blocking collectives: 130 us -> 116 us
    psum x1 -> x2, blocking collectives: 34.7 us -> 20.6 us  [the longest x1 12.6 us: group_the_region(): return lax.psum(back, chip_axis)]
where the time goes in v1:
time: 339 us; the launch traced here: 337 us
  blocking collectives  116 us (34%)
  waiting for transfers between devices  72.9 us (22%)
  starting transfers between devices  71.5 us (21%)
  local copies, waits for them, and re-layouts  26.9 us (8%)
  other arithmetic  26.3 us (8%)
  between operations  12.9 us (4%)
  matrix products  10.8 us (3%)
    psum x3, blocking collectives, two_products(): lax.psum((jnp.sum(residual * residual), jnp.sum(residual * image)), ('gx'...  91.4 us
    ppermute x18, waiting for transfers between devices, extended(): lax.ppermute(head, axis, [((i + 1) % count, i) for i in range(ends)])  55 us
    ppermute x18, starting transfers between devices, extended(): lax.ppermute(tail, axis, [(i, (i + 1) % count) for i in range(ends)])  33.7 us
    ppermute x18, starting transfers between devices, extended(): lax.ppermute(head, axis, [((i + 1) % count, i) for i in range(ends)])  23.5 us
    psum x1, blocking collectives, group_the_region(): return lax.psum(back, chip_axis)  12.6 us
    ppermute x18, waiting for transfers between devices, extended(): lax.ppermute(tail, axis, [(i, (i + 1) % count) for i in range(ends)])  10.4 us
    gather x4, local copies, waits for them, and re-layouts, per_group(): selected_entries = jnp.take(weights, block_tables, axis=0)  8.68 us
    dot_general x4, matrix products, per_group(): jnp.einsum('aow,awv->aov', block_coefficient_values, selected_entries, pr...  8.3 us
  transfers between devices with their start and end apart: 39, of which 25 were waited for; matrix products, arithmetic and copies ran while one was open for 4% of the time, Pallas kernels for 0%

profile of v1, /device:TPU:0, one launch (start us, length us, event | category | flops | bytes accessed | tf_op | source)
XLA Modules:
  0.0 337.0 jit_solution(11320903060627053850)
XLA Ops:
  3.7 7.3 %all-to-all-start.2 = ((s32[8,1,16]{2,1,0:T(1,128)}), s32[8,1,16]{2,1,0:T(1,128)S(1)}, u32[]{:S(2)}, u32[]{:S(2)}) async-start(s32[8,1,16]{2,1,0:T(1,128)} %bitcast.17), calls=%async_computation.2 | async-start | bytes 8192 | tf_op jit(solution)/shard_map/all_to_all | solution.py:151
  11.0 1.5 fusion.98
  12.5 1.8 multiply_reduce_fusion.4
  15.0 2.4 all-to-all-done.2
  17.4 3.6 %all-to-all-start = ((s32[8,1,16]{2,1,0:T(1,128)}), s32[8,1,16]{2,1,0:T(1,128)S(1)}, u32[]{:S(2)}, u32[]{:S(2)}) async-start(s32[8,1,16]{2,1,0:T(1,128)} %bitcast.8), calls=%async_computation | async-start | bytes 8192 | tf_op jit(solution)/shard_map/all_to_all | solution.py:152
  22.3 5.1 %all-to-all-done = s32[8,1,16]{2,1,0:T(1,128)S(1)} async-done(((s32[8,1,16]{2,1,0:T(1,128)}), s32[8,1,16]{2,1,0:T(1,128)S(1)}, u32[]{:S(2)}, u32[]{:S(2)}) %all-to-all-start) | async-done | bytes 544 | tf_op jit(solution)/shard_map/all_to_all | solution.py:152
  27.4 3.5 %all-to-all-start.1 = ((f32[8,16,4,256]{3,1,2,0:T(8,128)}), f32[8,16,4,256]{3,1,2,0:T(8,128)S(1)}, u32[]{:S(2)}, u32[]{:S(2)}) async-start(f32[8,16,4,256]{3,1,2,0:T(8,128)} %copy.111), calls=%async_computation.1 | async-start | bytes 1048576 | tf_op jit(solution)/shard_map/all_to_all | solution.py:150
  30.9 8.0 %all-reduce.3 = (f32[]{:T(128)}, f32[]{:T(128)}) all-reduce(f32[]{:T(128)} %get-tuple-element.66, f32[]{:T(128)} %get-tuple-element.64), channel_id=1, replica_groups=mesh['grp'=2,'gx'=4,'gy'=2,'gz'=2] {'gy','gz'}, use_global_device_ids=true, to_apply=%region_1.0 | all-reduce | flops 2 | bytes 16 | tf_op jit(solution)/shard_map/psum | solution.py:18
  38.9 12.6 %all-reduce.4 = (f32[]{:T(128)}, f32[]{:T(128)}) all-reduce(f32[]{:T(128)} %get-tuple-element.60, f32[]{:T(128)} %get-tuple-element.61), channel_id=1, replica_groups=mesh['grp'=2,'gx'=4,'gy'=2,'gz'=2] {'gx'}, use_global_device_ids=true, to_apply=%region_2.0 | all-reduce | flops 2 | bytes 16 | tf_op jit(solution)/shard_map/psum | solution.py:19
  56.3 17.2 %while.10 = (s32[]{:T(128)}, f32[4,32,3,128]{3,2,1,0:T(4,128)S(1)}, bf16[4,32,3,256]{3,2,1,0:T(4,128)(2,1)S(1)}, s32[4,32]{1,0:T(4,128)S(1)}, bf16[32,256,128]{2,1,0:T(8,128)(2,1)S(1)}, /*index=5*/s32[]{:T(128)}) while((s32[]{:T(128)}, f32[4,32,3,128]{3,2,1,0:T(4,128)S(1)}, bf16[4,32,3,256]{3,2,1,0:T(4,128)(2,1)S(1)}, ...), condition=%wide.region_10.11_spmd, body=%wide.region_9.10_spmd.sunk | while | flops 7341346 | bytes 6428917 | solution.py:95
  56.4 2.2 gather_fusion
  58.6 2.1 fusion.120
  60.7 2.2 gather_fusion
  62.9 2.1 fusion.120
  65.0 2.2 gather_fusion
  67.2 2.1 fusion.120
  69.3 2.2 gather_fusion
  71.5 2.1 fusion.120
  74.9 3.5 %psum.81 = f32[3,32,128]{2,1,0:T(8,128)S(1)} all-reduce(f32[3,32,128]{2,1,0:T(8,128)S(1)} %reshape.93), channel_id=1, replica_groups=mesh['grp'=2,'gx'=4,'gy'=2,'gz'=2] {'gz'}, use_global_device_ids=true, to_apply=%region_11.12 | all-reduce | flops 12288 | bytes 98304 | tf_op jit(solution)/shard_map/psum | solution.py:168
  79.9 1.3 collective-permute-start.1
  81.4 4.2 %collective-permute-done.1 = f32[3,16,1,128]{3,1,2,0:T(8,128)S(1)} collective-permute-done((f32[3,16,1,128]{3,1,2,0:T(8,128)S(1)}, f32[3,16,1,128]{3,1,2,0:T(8,128)S(1)}, u32[]{:S(2)}, u32[]{:S(2)}) %collective-permute-start.1) | collective-permute-done | bytes 24608 | tf_op jit(solution)/shard_map/ppermute | solution.py:35
  86.4 2.4 collective-permute-start.2
  91.1 3.9 %collective-permute-done.3 = f32[3,16,34,1]{2,1,3,0:T(8,128)S(1)} collective-permute-done((f32[3,16,34,1]{2,1,3,0:T(8,128)S(1)}, f32[3,16,34,1]{2,1,3,0:T(8,128)S(1)}, u32[]{:S(2)}, u32[]{:S(2)}) %collective-permute-start.3) | collective-permute-done | bytes 6560 | tf_op jit(solution)/shard_map/ppermute | solution.py:35
  96.2 1.3 collective-permute-start.4
  97.5 1.3 collective-permute-start.5
  98.8 1.9 collective-permute-done.5
  102.5 2.7 collective-permute-start.7
  105.2 1.3 collective-permute-start.6
  106.6 4.2 %collective-permute-done.6 = f32[16,1,128]{2,0,1:T(8,128)S(1)} collective-permute-done((f32[16,1,128]{2,0,1:T(8,128)S(1)}, f32[16,1,128]{2,0,1:T(8,128)S(1)}, u32[]{:S(2)}, u32[]{:S(2)}) %collective-permute-start.6) | collective-permute-done | bytes 8224 | tf_op jit(solution)/shard_map/ppermute | solution.py:35
  110.9 1.6 collective-permute-start.9
  112.6 1.3 collective-permute-start.8
  114.4 3.0 collective-permute-done.9
  117.4 4.1 %collective-permute-done.8 = f32[16,34,1]{2,0,1:T(8,128)S(1)} collective-permute-done((f32[16,34,1]{2,0,1:T(8,128)S(1)}, f32[16,34,1]{2,0,1:T(8,128)S(1)}, u32[]{:S(2)}, u32[]{:S(2)}) %collective-permute-start.8) | collective-permute-done | bytes 2208 | tf_op jit(solution)/shard_map/ppermute | solution.py:35
  123.1 3.3 collective-permute-start.11
  128.8 30.5 %all-reduce.2 = (f32[]{:T(128)}, f32[]{:T(128)}) all-reduce(f32[]{:T(128)} %get-tuple-element.41, f32[]{:T(128)} %get-tuple-element.40), channel_id=1, replica_groups=mesh['grp'=2,'gx'=4,'gy'=2,'gz'=2] {'gx','gy','gz'}, use_global_device_ids=true, to_apply=%region_13.14 | all-reduce | flops 2 | bytes 16 | tf_op jit(solution)/shard_map/psum | solution.py:100
  162.0 1.3 collective-permute-start.13
  163.5 4.2 %collective-permute-done.13 = f32[3,16,1,128]{3,1,2,0:T(8,128)S(1)} collective-permute-done((f32[3,16,1,128]{3,1,2,0:T(8,128)S(1)}, f32[3,16,1,128]{3,1,2,0:T(8,128)S(1)}, u32[]{:S(2)}, u32[]{:S(2)}) %collective-permute-start.13) | collective-permute-done | bytes 24608 | tf_op jit(solution)/shard_map/ppermute | solution.py:35
  173.3 4.0 %collective-permute-done.15 = f32[3,16,34,1]{2,1,3,0:T(8,128)} collective-permute-done((f32[3,16,34,1]{2,1,3,0:T(8,128)S(1)}, f32[3,16,34,1]{2,1,3,0:T(8,128)}, u32[]{:S(2)}, u32[]{:S(2)}) %collective-permute-start.15) | collective-permute-done | bytes 6560 | tf_op jit(solution)/shard_map/ppermute | solution.py:35
  178.6 1.5 pad_maximum_fusion.75
  180.1 1.3 collective-permute-start.16
  181.4 1.3 collective-permute-start.17
  182.7 1.9 collective-permute-done.17
  186.4 2.0 collective-permute-start.19
  189.7 4.2 %collective-permute-done.18 = f32[16,1,128]{2,0,1:T(8,128)S(1)} collective-permute-done((f32[16,1,128]{2,0,1:T(8,128)S(1)}, f32[16,1,128]{2,0,1:T(8,128)S(1)}, u32[]{:S(2)}, u32[]{:S(2)}) %collective-permute-start.18) | collective-permute-done | bytes 8224 | tf_op jit(solution)/shard_map/ppermute | solution.py:35
  194.1 1.5 collective-permute-start.21
  197.4 3.1 collective-permute-done.21
  200.5 4.1 %collective-permute-done.20 = f32[16,34,1]{2,0,1:T(8,128)S(1)} collective-permute-done((f32[16,34,1]{2,0,1:T(8,128)S(1)}, f32[16,34,1]{2,0,1:T(8,128)S(1)}, u32[]{:S(2)}, u32[]{:S(2)}) %collective-permute-start.20) | collective-permute-done | bytes 2208 | tf_op jit(solution)/shard_map/ppermute | solution.py:35
  206.2 3.2 collective-permute-start.23
  212.0 30.5 %all-reduce.1 = (f32[]{:T(128)}, f32[]{:T(128)}) all-reduce(f32[]{:T(128)} %get-tuple-element.39, f32[]{:T(128)} %get-tuple-element.38), channel_id=1, replica_groups=mesh['grp'=2,'gx'=4,'gy'=2,'gz'=2] {'gx','gy','gz'}, use_global_device_ids=true, to_apply=%region_17.18 | all-reduce | flops 2 | bytes 16 | tf_op jit(solution)/shard_map/psum | solution.py:100
  250.3 4.2 %collective-permute-done.25 = f32[3,16,1,128]{3,1,2,0:T(8,128)S(1)} collective-permute-done((f32[3,16,1,128]{3,1,2,0:T(8,128)S(1)}, f32[3,16,1,128]{3,1,2,0:T(8,128)S(1)}, u32[]{:S(2)}, u32[]{:S(2)}) %collective-permute-start.25) | collective-permute-done | bytes 24608 | tf_op jit(solution)/shard_map/ppermute | solution.py:35
  255.8 1.6 copy.139
  259.1 1.5 collective-permute-start.27
  261.2 3.8 %collective-permute-done.27 = f32[3,16,34,1]{2,1,3,0:T(8,128)} collective-permute-done((f32[3,16,34,1]{2,1,3,0:T(8,128)S(1)}, f32[3,16,34,1]{2,1,3,0:T(8,128)}, u32[]{:S(2)}, u32[]{:S(2)}) %collective-permute-start.27) | collective-permute-done | bytes 6560 | tf_op jit(solution)/shard_map/ppermute | solution.py:35
  266.2 1.5 pad_maximum_fusion.70
  267.7 1.3 collective-permute-start.28
  270.3 1.9 collective-permute-done.29
  274.0 2.0 collective-permute-start.31
  277.3 4.2 %collective-permute-done.30 = f32[16,1,128]{2,0,1:T(8,128)S(1)} collective-permute-done((f32[16,1,128]{2,0,1:T(8,128)S(1)}, f32[16,1,128]{2,0,1:T(8,128)S(1)}, u32[]{:S(2)}, u32[]{:S(2)}) %collective-permute-start.30) | collective-permute-done | bytes 8224 | tf_op jit(solution)/shard_map/ppermute | solution.py:35
  281.7 1.5 collective-permute-start.33
  283.2 1.3 collective-permute-start.32
  285.0 3.1 collective-permute-done.33
  288.1 4.1 %collective-permute-done.32 = f32[16,34,1]{2,0,1:T(8,128)S(1)} collective-permute-done((f32[16,34,1]{2,0,1:T(8,128)S(1)}, f32[16,34,1]{2,0,1:T(8,128)S(1)}, u32[]{:S(2)}, u32[]{:S(2)}) %collective-permute-start.32) | collective-permute-done | bytes 2208 | tf_op jit(solution)/shard_map/ppermute | solution.py:35
  293.9 3.2 collective-permute-start.35
  299.7 30.4 %all-reduce = (f32[]{:T(128)}, f32[]{:T(128)}) all-reduce(f32[]{:T(128)} %get-tuple-element.37, f32[]{:T(128)} %get-tuple-element.36), channel_id=1, replica_groups=mesh['grp'=2,'gx'=4,'gy'=2,'gz'=2] {'gx','gy','gz'}, use_global_device_ids=true, to_apply=%region_21.22 | all-reduce | flops 2 | bytes 16 | tf_op jit(solution)/shard_map/psum | solution.py:100
  (163 shorter events, 59.5 us)
Async XLA Ops:
  0.6 54.6 %copy-start = (f32[4,3]{1,0:T(4,128)S(1)}, f32[4,3]{1,0:T(4,128)}, u32[]{:S(2)}) copy-start(f32[4,3]{1,0:T(4,128)} %param.20) | copy-start | bytes 148
  0.6 52.1 %copy-start.17 = (f32[16]{0:T(128)S(1)}, f32[16]{0:T(128)}, u32[]{:S(2)}) copy-start(f32[16]{0:T(128)} %param.22) | copy-start | bytes 196
  3.7 13.7 %all-to-all-start.2 = ((s32[8,1,16]{2,1,0:T(1,128)}), s32[8,1,16]{2,1,0:T(1,128)S(1)}, u32[]{:S(2)}, u32[]{:S(2)}) async-start(s32[8,1,16]{2,1,0:T(1,128)} %bitcast.17), calls=%async_computation.2 | async-start | bytes 8192 | tf_op jit(solution)/shard_map/all_to_all | solution.py:151
  14.3 42.0 %copy-start.1 = (bf16[32,256,128]{2,1,0:T(8,128)(2,1)S(1)}, bf16[32,256,128]{2,1,0:T(8,128)(2,1)}, u32[]{:S(2)}) copy-start(bf16[32,256,128]{2,1,0:T(8,128)(2,1)} %param.21) | copy-start | bytes 6291460
  17.4 10.0 %all-to-all-start = ((s32[8,1,16]{2,1,0:T(1,128)}), s32[8,1,16]{2,1,0:T(1,128)S(1)}, u32[]{:S(2)}, u32[]{:S(2)}) async-start(s32[8,1,16]{2,1,0:T(1,128)} %bitcast.8), calls=%async_computation | async-start | bytes 8192 | tf_op jit(solution)/shard_map/all_to_all | solution.py:152
  27.4 27.5 %all-to-all-start.1 = ((f32[8,16,4,256]{3,1,2,0:T(8,128)}), f32[8,16,4,256]{3,1,2,0:T(8,128)S(1)}, u32[]{:S(2)}, u32[]{:S(2)}) async-start(f32[8,16,4,256]{3,1,2,0:T(8,128)} %copy.111), calls=%async_computation.1 | async-start | bytes 1048576 | tf_op jit(solution)/shard_map/all_to_all | solution.py:150
  78.4 7.5 %copy-start.9 = (f32[3,32,128]{2,1,0:T(8,128)}, f32[3,32,128]{2,1,0:T(8,128)S(1)}, u32[]{:S(2)}) copy-start(f32[3,32,128]{2,1,0:T(8,128)S(1)} %psum.81) | copy-start | bytes 147460
  78.6 2.8 collective-permute-start
  79.9 5.7 %collective-permute-start.1 = (f32[3,16,1,128]{3,1,2,0:T(8,128)S(1)}, f32[3,16,1,128]{3,1,2,0:T(8,128)S(1)}, u32[]{:S(2)}, u32[]{:S(2)}) collective-permute-start(f32[3,16,1,128]{3,1,2,0:T(8,128)S(1)} %get-tuple-element.102), channel_id=1, source_target_pairs={{4,0},{8,4},{12,8},{5,1},{9,5},{13,9},{6,2},{10,6},{14,10},{7,3},{... | collective-permute-start | bytes 73736 | tf_op jit(solution)/shard_map/ppermute | solution.py:35
  86.4 4.2 %collective-permute-start.2 = (f32[3,16,34,1]{2,1,3,0:T(8,128)S(1)}, f32[3,16,34,1]{2,1,3,0:T(8,128)S(1)}, u32[]{:S(2)}, u32[]{:S(2)}) collective-permute-start(f32[3,16,34,1]{2,1,3,0:T(8,128)S(1)} %copy.135), channel_id=1, source_target_pairs={{0,2},{1,3},{4,6},{5,7},{8,10},{9,11},{12,14},{13,15},{16,18},{17,... | collective-permute-start | bytes 19592 | tf_op jit(solution)/shard_map/ppermute | solution.py:33
  89.3 5.7 %collective-permute-start.3 = (f32[3,16,34,1]{2,1,3,0:T(8,128)S(1)}, f32[3,16,34,1]{2,1,3,0:T(8,128)S(1)}, u32[]{:S(2)}, u32[]{:S(2)}) collective-permute-start(f32[3,16,34,1]{2,1,3,0:T(8,128)S(1)} %copy.136), channel_id=1, source_target_pairs={{2,0},{3,1},{6,4},{7,5},{10,8},{11,9},{14,12},{15,13},{18,16},{19,... | collective-permute-start | bytes 19592 | tf_op jit(solution)/shard_map/ppermute | solution.py:35
  96.2 2.6 collective-permute-start.4
  97.5 3.2 collective-permute-start.5
  102.0 11.8 %copy-start.2 = (f32[16,32,128]{2,1,0:T(8,128)S(1)}, f32[16,32,128]{2,1,0:T(8,128)}, u32[]{:S(2)}) copy-start(f32[16,32,128]{2,1,0:T(8,128)} %param.23) | copy-start | bytes 786436
  102.5 4.1 %collective-permute-start.7 = (f32[16,1,128]{2,0,1:T(8,128)S(1)}, f32[16,1,128]{2,0,1:T(8,128)S(1)}, u32[]{:S(2)}, u32[]{:S(2)}) collective-permute-start(f32[16,1,128]{2,0,1:T(8,128)S(1)} %get-tuple-element.113), channel_id=1, source_target_pairs={{0,4},{4,8},{8,12},{1,5},{5,9},{9,13},{2,6},{6,10},{10,14},{3,7},{... | collective-permute-start | bytes 24584 | tf_op jit(solution)/shard_map/ppermute | solution.py:33
  105.2 5.5 %collective-permute-start.6 = (f32[16,1,128]{2,0,1:T(8,128)S(1)}, f32[16,1,128]{2,0,1:T(8,128)S(1)}, u32[]{:S(2)}, u32[]{:S(2)}) collective-permute-start(f32[16,1,128]{2,0,1:T(8,128)S(1)} %get-tuple-element.114), channel_id=1, source_target_pairs={{4,0},{8,4},{12,8},{5,1},{9,5},{13,9},{6,2},{10,6},{14,10},{7,3},{... | collective-permute-start | bytes 24584 | tf_op jit(solution)/shard_map/ppermute | solution.py:35
  110.9 6.4 %collective-permute-start.9 = (f32[16,34,1]{2,0,1:T(8,128)S(1)}, f32[16,34,1]{2,0,1:T(8,128)S(1)}, u32[]{:S(2)}, u32[]{:S(2)}) collective-permute-start(f32[16,34,1]{2,0,1:T(8,128)S(1)} %get-tuple-element.107), channel_id=1, source_target_pairs={{0,2},{1,3},{4,6},{5,7},{8,10},{9,11},{12,14},{13,15},{16,18},{17,... | collective-permute-start | bytes 6536 | tf_op jit(solution)/shard_map/ppermute | solution.py:33
  112.6 8.9 %collective-permute-start.8 = (f32[16,34,1]{2,0,1:T(8,128)S(1)}, f32[16,34,1]{2,0,1:T(8,128)S(1)}, u32[]{:S(2)}, u32[]{:S(2)}) collective-permute-start(f32[16,34,1]{2,0,1:T(8,128)S(1)} %get-tuple-element.108), channel_id=1, source_target_pairs={{2,0},{3,1},{6,4},{7,5},{10,8},{11,9},{14,12},{15,13},{18,16},{19,... | collective-permute-start | bytes 6536 | tf_op jit(solution)/shard_map/ppermute | solution.py:35
  121.8 5.3 %collective-permute-start.10 = (f32[1,34,130]{2,0,1:T(1,128)S(1)}, f32[1,34,130]{2,0,1:T(1,128)S(1)}, u32[]{:S(2)}, u32[]{:S(2)}) collective-permute-start(f32[1,34,130]{2,0,1:T(1,128)S(1)} %get-tuple-element.91), channel_id=1, source_target_pairs={{1,0},{3,2},{5,4},{7,6},{9,8},{11,10},{13,12},{15,14},{17,16},{19,... | collective-permute-start | bytes 53048 | tf_op jit(solution)/shard_map/ppermute | solution.py:35
  123.1 4.7 %copy-start.10 = (f32[3,32,128]{2,1,0:T(8,128)S(1)}, f32[3,32,128]{2,1,0:T(8,128)}, u32[]{:S(2)}) copy-start(f32[3,32,128]{2,1,0:T(8,128)} %copy-done.9) | copy-start | bytes 147460
  123.1 4.0 %collective-permute-start.11 = (f32[1,34,130]{2,0,1:T(1,128)S(1)}, f32[1,34,130]{2,0,1:T(1,128)S(1)}, u32[]{:S(2)}, u32[]{:S(2)}) collective-permute-start(f32[1,34,130]{2,0,1:T(1,128)S(1)} %get-tuple-element.92), channel_id=1, source_target_pairs={{0,1},{2,3},{4,5},{6,7},{8,9},{10,11},{12,13},{14,15},{16,17},{18,... | collective-permute-start | bytes 53048 | tf_op jit(solution)/shard_map/ppermute | solution.py:33
  160.7 2.8 collective-permute-start.12
  162.0 5.7 %collective-permute-start.13 = (f32[3,16,1,128]{3,1,2,0:T(8,128)S(1)}, f32[3,16,1,128]{3,1,2,0:T(8,128)S(1)}, u32[]{:S(2)}, u32[]{:S(2)}) collective-permute-start(f32[3,16,1,128]{3,1,2,0:T(8,128)S(1)} %get-tuple-element.100), channel_id=1, source_target_pairs={{4,0},{8,4},{12,8},{5,1},{9,5},{13,9},{6,2},{10,6},{14,10},{7,3},{... | collective-permute-start | bytes 73736 | tf_op jit(solution)/shard_map/ppermute | solution.py:35
  167.7 0.6 copy-start.13
  169.7 3.0 collective-permute-start.14
  171.5 5.8 %collective-permute-start.15 = (f32[3,16,34,1]{2,1,3,0:T(8,128)S(1)}, f32[3,16,34,1]{2,1,3,0:T(8,128)}, u32[]{:S(2)}, u32[]{:S(2)}) collective-permute-start(f32[3,16,34,1]{2,1,3,0:T(8,128)S(1)} %copy.138), channel_id=1, source_target_pairs={{2,0},{3,1},{6,4},{7,5},{10,8},{11,9},{14,12},{15,13},{18,16},{19,... | collective-permute-start | bytes 19592 | tf_op jit(solution)/shard_map/ppermute | solution.py:35
  178.5 6.0 %copy-start.14 = (f32[3,16,1,128]{3,1,2,0:T(8,128)S(1)}, f32[3,16,1,128]{3,1,2,0:T(8,128)}, u32[]{:S(2)}) copy-start(f32[3,16,1,128]{3,1,2,0:T(8,128)} %copy-done.13) | copy-start | bytes 73732
  180.1 2.6 collective-permute-start.16
  181.4 3.2 collective-permute-start.17
  186.4 3.3 collective-permute-start.19
  188.3 5.5 %collective-permute-start.18 = (f32[16,1,128]{2,0,1:T(8,128)S(1)}, f32[16,1,128]{2,0,1:T(8,128)S(1)}, u32[]{:S(2)}, u32[]{:S(2)}) collective-permute-start(f32[16,1,128]{2,0,1:T(8,128)S(1)} %get-tuple-element.112), channel_id=1, source_target_pairs={{4,0},{8,4},{12,8},{5,1},{9,5},{13,9},{6,2},{10,6},{14,10},{7,3},{... | collective-permute-start | bytes 24584 | tf_op jit(solution)/shard_map/ppermute | solution.py:35
  194.1 6.5 %collective-permute-start.21 = (f32[16,34,1]{2,0,1:T(8,128)S(1)}, f32[16,34,1]{2,0,1:T(8,128)S(1)}, u32[]{:S(2)}, u32[]{:S(2)}) collective-permute-start(f32[16,34,1]{2,0,1:T(8,128)S(1)} %get-tuple-element.105), channel_id=1, source_target_pairs={{0,2},{1,3},{4,6},{5,7},{8,10},{9,11},{12,14},{13,15},{16,18},{17,... | collective-permute-start | bytes 6536 | tf_op jit(solution)/shard_map/ppermute | solution.py:33
  195.6 9.0 %collective-permute-start.20 = (f32[16,34,1]{2,0,1:T(8,128)S(1)}, f32[16,34,1]{2,0,1:T(8,128)S(1)}, u32[]{:S(2)}, u32[]{:S(2)}) collective-permute-start(f32[16,34,1]{2,0,1:T(8,128)S(1)} %get-tuple-element.106), channel_id=1, source_target_pairs={{2,0},{3,1},{6,4},{7,5},{10,8},{11,9},{14,12},{15,13},{18,16},{19,... | collective-permute-start | bytes 6536 | tf_op jit(solution)/shard_map/ppermute | solution.py:35
  197.4 49.9 %copy-start.3 = (f32[1,16,32,128]{3,1,2,0:T(8,128)}, f32[1,16,32,128]{3,1,2,0:T(8,128)S(1)}, u32[]{:S(2)}) copy-start(f32[1,16,32,128]{3,1,2,0:T(8,128)S(1)} %fusion.59) | copy-start | bytes 786436
  204.9 5.1 %collective-permute-start.22 = (f32[1,34,130]{2,0,1:T(1,128)S(1)}, f32[1,34,130]{2,0,1:T(1,128)S(1)}, u32[]{:S(2)}, u32[]{:S(2)}) collective-permute-start(f32[1,34,130]{2,0,1:T(1,128)S(1)} %get-tuple-element.87), channel_id=1, source_target_pairs={{1,0},{3,2},{5,4},{7,6},{9,8},{11,10},{13,12},{15,14},{17,16},{19,... | collective-permute-start | bytes 53048 | tf_op jit(solution)/shard_map/ppermute | solution.py:35
  206.2 4.7 %copy-start.11 = (f32[3,32,128]{2,1,0:T(8,128)S(1)}, f32[3,32,128]{2,1,0:T(8,128)}, u32[]{:S(2)}) copy-start(f32[3,32,128]{2,1,0:T(8,128)} %copy-done.9) | copy-start | bytes 147460
  206.2 4.0 %collective-permute-start.23 = (f32[1,34,130]{2,0,1:T(1,128)S(1)}, f32[1,34,130]{2,0,1:T(1,128)S(1)}, u32[]{:S(2)}, u32[]{:S(2)}) collective-permute-start(f32[1,34,130]{2,0,1:T(1,128)S(1)} %get-tuple-element.88), channel_id=1, source_target_pairs={{0,1},{2,3},{4,5},{6,7},{8,9},{10,11},{12,13},{14,15},{16,17},{18,... | collective-permute-start | bytes 53048 | tf_op jit(solution)/shard_map/ppermute | solution.py:33
  210.1 37.4 %copy-start.5 = (f32[1,16,32,128]{3,1,2,0:T(8,128)}, f32[1,16,32,128]{3,1,2,0:T(8,128)S(1)}, u32[]{:S(2)}) copy-start(f32[1,16,32,128]{3,1,2,0:T(8,128)S(1)} %fusion.51) | copy-start | bytes 786436
  210.9 43.7 %copy-start.7 = (f32[1,16,32,128]{3,1,2,0:T(8,128)}, f32[1,16,32,128]{3,1,2,0:T(8,128)S(1)}, u32[]{:S(2)}) copy-start(f32[1,16,32,128]{3,1,2,0:T(8,128)S(1)} %fusion.45) | copy-start | bytes 786436
  247.5 2.8 collective-permute-start.24
  248.8 5.7 %collective-permute-start.25 = (f32[3,16,1,128]{3,1,2,0:T(8,128)S(1)}, f32[3,16,1,128]{3,1,2,0:T(8,128)S(1)}, u32[]{:S(2)}, u32[]{:S(2)}) collective-permute-start(f32[3,16,1,128]{3,1,2,0:T(8,128)S(1)} %get-tuple-element.98), channel_id=1, source_target_pairs={{4,0},{8,4},{12,8},{5,1},{9,5},{13,9},{6,2},{10,6},{14,10},{7,3},{... | collective-permute-start | bytes 73736 | tf_op jit(solution)/shard_map/ppermute | solution.py:35
  254.5 1.3 copy-start.15
  257.4 3.3 collective-permute-start.26
  259.1 5.8 %collective-permute-start.27 = (f32[3,16,34,1]{2,1,3,0:T(8,128)S(1)}, f32[3,16,34,1]{2,1,3,0:T(8,128)}, u32[]{:S(2)}, u32[]{:S(2)}) collective-permute-start(f32[3,16,34,1]{2,1,3,0:T(8,128)S(1)} %copy.140), channel_id=1, source_target_pairs={{2,0},{3,1},{6,4},{7,5},{10,8},{11,9},{14,12},{15,13},{18,16},{19,... | collective-permute-start | bytes 19592 | tf_op jit(solution)/shard_map/ppermute | solution.py:35
  266.2 6.0 %copy-start.16 = (f32[3,16,1,128]{3,1,2,0:T(8,128)S(1)}, f32[3,16,1,128]{3,1,2,0:T(8,128)}, u32[]{:S(2)}) copy-start(f32[3,16,1,128]{3,1,2,0:T(8,128)} %copy-done.15) | copy-start | bytes 73732
  267.7 2.6 collective-permute-start.28
  269.0 3.2 collective-permute-start.29
  274.0 3.3 collective-permute-start.31
  276.0 5.5 %collective-permute-start.30 = (f32[16,1,128]{2,0,1:T(8,128)S(1)}, f32[16,1,128]{2,0,1:T(8,128)S(1)}, u32[]{:S(2)}, u32[]{:S(2)}) collective-permute-start(f32[16,1,128]{2,0,1:T(8,128)S(1)} %get-tuple-element.110), channel_id=1, source_target_pairs={{4,0},{8,4},{12,8},{5,1},{9,5},{13,9},{6,2},{10,6},{14,10},{7,3},{... | collective-permute-start | bytes 24584 | tf_op jit(solution)/shard_map/ppermute | solution.py:35
  281.7 6.4 %collective-permute-start.33 = (f32[16,34,1]{2,0,1:T(8,128)S(1)}, f32[16,34,1]{2,0,1:T(8,128)S(1)}, u32[]{:S(2)}, u32[]{:S(2)}) collective-permute-start(f32[16,34,1]{2,0,1:T(8,128)S(1)} %get-tuple-element.103), channel_id=1, source_target_pairs={{0,2},{1,3},{4,6},{5,7},{8,10},{9,11},{12,14},{13,15},{16,18},{17,... | collective-permute-start | bytes 6536 | tf_op jit(solution)/shard_map/ppermute | solution.py:33
  283.2 9.0 %collective-permute-start.32 = (f32[16,34,1]{2,0,1:T(8,128)S(1)}, f32[16,34,1]{2,0,1:T(8,128)S(1)}, u32[]{:S(2)}, u32[]{:S(2)}) collective-permute-start(f32[16,34,1]{2,0,1:T(8,128)S(1)} %get-tuple-element.104), channel_id=1, source_target_pairs={{2,0},{3,1},{6,4},{7,5},{10,8},{11,9},{14,12},{15,13},{18,16},{19,... | collective-permute-start | bytes 6536 | tf_op jit(solution)/shard_map/ppermute | solution.py:35
  292.6 5.2 %collective-permute-start.34 = (f32[1,34,130]{2,0,1:T(1,128)S(1)}, f32[1,34,130]{2,0,1:T(1,128)S(1)}, u32[]{:S(2)}, u32[]{:S(2)}) collective-permute-start(f32[1,34,130]{2,0,1:T(1,128)S(1)} %get-tuple-element.83), channel_id=1, source_target_pairs={{1,0},{3,2},{5,4},{7,6},{9,8},{11,10},{13,12},{15,14},{17,16},{19,... | collective-permute-start | bytes 53048 | tf_op jit(solution)/shard_map/ppermute | solution.py:35
  293.9 4.7 %copy-start.4 = (f32[1,16,32,128]{3,1,2,0:T(8,128)S(1)}, f32[1,16,32,128]{3,1,2,0:T(8,128)}, u32[]{:S(2)}) copy-start(f32[1,16,32,128]{3,1,2,0:T(8,128)} %copy-done.3) | copy-start | bytes 786436
  293.9 4.7 %copy-start.6 = (f32[1,16,32,128]{3,1,2,0:T(8,128)S(1)}, f32[1,16,32,128]{3,1,2,0:T(8,128)}, u32[]{:S(2)}) copy-start(f32[1,16,32,128]{3,1,2,0:T(8,128)} %copy-done.5) | copy-start | bytes 786436
  293.9 4.7 %copy-start.8 = (f32[1,16,32,128]{3,1,2,0:T(8,128)S(1)}, f32[1,16,32,128]{3,1,2,0:T(8,128)}, u32[]{:S(2)}) copy-start(f32[1,16,32,128]{3,1,2,0:T(8,128)} %copy-done.7) | copy-start | bytes 786436
  293.9 4.7 %copy-start.12 = (f32[3,32,128]{2,1,0:T(8,128)S(1)}, f32[3,32,128]{2,1,0:T(8,128)}, u32[]{:S(2)}) copy-start(f32[3,32,128]{2,1,0:T(8,128)} %copy-done.9) | copy-start | bytes 147460
  293.9 4.0 %collective-permute-start.35 = (f32[1,34,130]{2,0,1:T(1,128)S(1)}, f32[1,34,130]{2,0,1:T(1,128)S(1)}, u32[]{:S(2)}, u32[]{:S(2)}) collective-permute-start(f32[1,34,130]{2,0,1:T(1,128)S(1)} %get-tuple-element.84), channel_id=1, source_target_pairs={{0,1},{2,3},{4,5},{6,7},{8,9},{10,11},{12,13},{14,15},{16,17},{18,... | collective-permute-start | bytes 53048 | tf_op jit(solution)/shard_map/ppermute | solution.py:33
